TPU v7x, 128 devices: a whole 4x4x4 slice. The times are simulated.
128 devices in a mesh: dp: 1, vp: 128 (over z, y, x, core).
Axes of the slice: x: 4, y: 4, z: 4, core: 2. Of those that a mesh axis runs over, the one named last changes fastest.
Arguments:
- hidden: bfloat16 [8192, 3584], P(('dp', 'vp'))
- target: int32 [8192], P('dp')
- norm_gain: bfloat16 [3584], replicated
- head_weight: bfloat16 [3584, 151936], P(None, 'vp')
Outputs:
- output 1: float32 [8192], P('dp')
- output 2: float32 [8192], P('dp')
- output 3: float32 [1], P('dp')
All inputs are finite; a program needn't handle non-finite values.
Results may differ from a plain program's by a relative error of at most 0.001.
Values are sent between devices in bfloat16 or wider.
A program may use at most 1 GiB of HBM per device.

v0:
```python
import jax
import jax.numpy as jnp
from jax import lax
from jax.sharding import PartitionSpec as P

NORM_EPS = 1e-6


def solution(mesh):
    def local_step(hidden, target, norm_gain, head_weight):
        hidden_f32 = hidden.astype(jnp.float32)
        inv_rms = lax.rsqrt(jnp.mean(hidden_f32 * hidden_f32, axis=-1, keepdims=True) + NORM_EPS)
        normed = (hidden_f32 * inv_rms * norm_gain.astype(jnp.float32)).astype(jnp.bfloat16)
        group_rows = lax.all_gather(normed, "vp", axis=0, tiled=True)
        logits = jnp.dot(group_rows, head_weight, preferred_element_type=jnp.float32)
        vocab_local = head_weight.shape[1]
        local_ids = target - lax.axis_index("vp") * vocab_local
        row_max = lax.pmax(jnp.max(logits, axis=-1), "vp")
        shifted = logits - row_max[:, None]
        exp_vals = jnp.exp(shifted)
        col_ids = jnp.arange(vocab_local, dtype=jnp.int32)
        target_shift = jnp.sum(jnp.where(col_ids[None, :] == local_ids[:, None], shifted, 0.0), axis=-1)
        local_stats = jnp.stack([jnp.sum(exp_vals, axis=-1), jnp.sum(exp_vals * shifted, axis=-1), target_shift])
        row_stats = lax.psum(local_stats, "vp")
        log_total = jnp.log(row_stats[0])
        log_prob = row_stats[2] - log_total
        entropy = log_total - row_stats[1] / row_stats[0]
        return log_prob, entropy, jnp.mean(log_prob).reshape(1)

    return jax.shard_map(local_step, mesh=mesh, in_specs=(P(("dp", "vp"), None), P("dp"), P(None), P(None, "vp")), out_specs=(P("dp"), P("dp"), P("dp")), check_vma=False)
```

profile of v0, /device:TPU:1, one launch (start us, length us, event | category | flops | bytes accessed | tf_op | source)
XLA Modules:
  0.0 484.5 jit_solution(5456235178380342283)
XLA Ops:
  7.2 0.0 all-gather.2.cloned.1.call-start
  7.2 0.7 convert_element_type.10
  7.9 1.2 fusion.1
  9.1 2.0 fusion.3
  11.1 0.0 all-gather.2.cloned.1.call-update
  11.2 0.0 all-reduce.2.cloned.1.call-start
  11.2 0.8 broadcast_subtract_fusion
  12.0 152.2 %all-gather.2.cloned.1.call-done = bf16[8192,3584]{1,0:T(8,128)(2,1)} async-done(((bf16[64,3584]{1,0:T(8,128)(2,1)}), bf16[8192,3584]{1,0:T(8,128)(2,1)}) %all-gather.2.cloned.1.call-update) | async-done | bytes 58720272 | tf_op jit(solution)/shard_map/all_gather | solution.py:14
  164.2 80.8 %fusion.6 = (f32[8192]{0:T(1024)S(1)}, f32[8192,1187]{0,1:T(8,128)}) fusion(bf16[8192,3584]{1,0:T(8,128)(2,1)} %all-gather.2.cloned.1.call-done, bf16[3584,1187]{0,1:T(8,128)(2,1)} %param.7), kind=kOutput, calls=%fused_computation.18 | convolution fusion | flops 69710659584 | bytes 106157056 | tf_op jit(solution)/shard_map/dot_general | solution.py:15
  245.0 64.5 %pmax.7 = f32[8192]{0:T(1024)S(1)} all-reduce(f32[8192]{0:T(1024)S(1)} %get-tuple-element.9), channel_id=1, replica_groups=mesh['dp'=1,'vp'=128] {'vp'}, use_global_device_ids=true, to_apply=%region_2.0 | all-reduce | flops 8192 | bytes 65536 | tf_op jit(solution)/shard_map/pmax | solution.py:18
  309.4 19.8 %exponential_reduce_fusion = (f32[8192]{0:T(1024)S(1)}, f32[8192]{0:T(1024)S(1)}, f32[8192]{0:T(1024)S(1)}) fusion(f32[8192,1187]{0,1:T(8,128)} %get-tuple-element.10, f32[8192]{0:T(1024)S(1)} %pmax.7, s32[8192]{0:T(1024)S(1)} %broadcast_subtract_fusion), kind=kLoop, calls=%fused_computation.1 | loop fusion | flops 68042752 | bytes 39059456 | tf_op jit(solution)/shard_map/reduce_sum | solution.py:23
  329.3 0.7 pad_maximum_fusion
  330.0 0.0 all-reduce.2.cloned.1.call-update
  330.0 143.5 %all-reduce.2.cloned.1.call-done = f32[3,8192]{1,0:T(4,128)} async-done(((f32[3,8192]{1,0:T(4,128)}), f32[3,8192]{1,0:T(4,128)}) %all-reduce.2.cloned.1.call-update) | async-done | bytes 98320 | tf_op jit(solution)/shard_map/psum | solution.py:24
  473.5 2.4 fusion.5
  (1 shorter events, 0.0 us)
Async XLA Ops:
  7.2 157.0 %all-gather.2.cloned.1.call-start = ((), (), s32[]{:S(2)}) async-start(), calls=%async_computation | async-start | bytes 59179008 | tf_op jit(solution)/shard_map/all_gather | solution.py:14
  11.2 462.4 %all-reduce.2.cloned.1.call-start = ((), (), s32[]{:S(2)}) async-start(), calls=%async_computation.1 | async-start | bytes 262144 | tf_op jit(solution)/shard_map/psum | solution.py:24
Sparse Core Ops, SparseCore 0:
  11.3 152.8 all-gather.1
  330.1 143.3 all-reduce.1
where the time goes:
time: 485 us
  waiting for transfers between devices  296 us (61%)
  matrix products  80.8 us (17%)
  blocking collectives  64.5 us (13%)
  other arithmetic  27.6 us (6%)
  between operations  15.8 us (3%)
    all_gather x1, waiting for transfers between devices, local_step(): group_rows = lax.all_gather(normed, 'vp', axis=0, tiled=True)  152 us
    psum x1, waiting for transfers between devices, local_step(): row_stats = lax.psum(local_stats, 'vp')  144 us
    dot_general x1, matrix products, local_step(): jnp.dot(group_rows, head_weight, preferred_element_type=jnp.float32)  80.8 us
    pmax x1, blocking collectives, local_step(): row_max = lax.pmax(jnp.max(logits, axis=-1), 'vp')  64.5 us
    reduce_sum x1, other arithmetic, local_step(): jnp.sum(exp_vals, axis=-1)  19.8 us
  transfers between devices with their start and end apart: 2, of which 2 were waited for; matrix products, arithmetic and copies ran while one was open for 0% of the time, Pallas kernels for 0%

commit v1 on v0

v1 whole, which is shorter than its diff:
```python
import functools

import jax
import jax.numpy as jnp
from jax import lax
from jax.experimental import pallas as pl
from jax.experimental.pallas import tpu as pltpu
from jax.sharding import PartitionSpec as P

NORM_EPS = 1e-6
MESH = pl.DeviceIdType.MESH
SIDE = 4
CHIPS = SIDE**3
OWN = CHIPS - 1
LOW = -3.0e38
DIRS = ((1, 0, 0), (0, 1, 0), (0, 0, 1), (-1, 0, 0), (0, -1, 0), (0, 0, -1))
FULL = 10

TREE = (
    (0, 63, (1, 0, 0)), (1, 63, (0, 1, 0)), (2, 63, (0, 0, 1)), (3, 63, (3, 0, 0)), (4, 63, (0, 3, 0)), (5, 63, (0, 0, 3)),
    (0, 4, (1, 3, 0)), (1, 0, (1, 1, 0)), (2, 4, (0, 3, 1)), (3, 3, (2, 0, 0)), (4, 4, (0, 2, 0)), (5, 0, (1, 0, 3)),
    (0, 2, (1, 0, 1)), (1, 3, (3, 1, 0)), (2, 3, (3, 0, 1)), (3, 4, (3, 3, 0)), (4, 5, (0, 3, 3)), (5, 5, (0, 0, 2)),
    (0, 7, (2, 1, 0)), (1, 2, (0, 1, 1)), (2, 6, (1, 3, 1)), (3, 5, (3, 0, 3)), (4, 9, (2, 3, 0)), (5, 1, (0, 1, 3)),
    (0, 11, (2, 0, 3)), (1, 17, (0, 1, 2)), (2, 12, (1, 0, 2)), (3, 16, (3, 3, 3)), (4, 11, (1, 3, 3)), (5, 16, (0, 3, 2)),
    (0, 10, (1, 2, 0)), (1, 19, (0, 2, 1)), (2, 9, (2, 0, 1)), (3, 8, (3, 3, 1)), (4, 16, (0, 2, 3)), (5, 7, (1, 1, 3)),
    (0, 26, (2, 0, 2)), (1, 12, (1, 1, 1)), (2, 14, (3, 0, 2)), (3, 19, (3, 1, 1)), (4, 15, (3, 2, 0)), (5, 13, (3, 1, 3)),
    (0, 35, (2, 1, 3)), (1, 18, (2, 2, 0)), (2, 30, (1, 2, 1)), (3, 29, (3, 3, 2)), (4, 28, (1, 2, 3)), (5, 35, (1, 1, 2)),
    (0, 28, (2, 3, 3)), (1, 36, (2, 1, 2)), (2, 31, (0, 2, 2)), (3, 31, (3, 2, 1)), (4, 26, (1, 3, 2)), (5, 41, (3, 1, 2)),
    (0, 46, (2, 2, 3)), (1, 41, (3, 2, 3)), (2, 43, (2, 2, 1)), (3, 39, (2, 1, 1)), (4, 32, (2, 3, 1)), (5, 46, (1, 2, 2)),
    (0, 52, (2, 3, 2)), (1, 49, (2, 2, 2)), (2, 51, (3, 2, 2)),
)
HALVES = 2
EVENTS = HALVES * (FULL + 1)
AHEAD = 2


def pieces_of(event):
    slot = event // HALVES
    return range(6 * slot, min(6 * slot + 6, OWN))


def kernel(hidden_ref, gain_ref, target_ref, head_ref, lp_ref, ent_ref, mean_ref, x_ref, w_ref, z_ref, tgt_ref, pack_ref,
           mine_ref, stat_ref, res_ref, fin_ref, peer_ref, send_sem, recv_sem, w_sem, w_send, w_recv, stat_send, stat_recv,
           fin_send, fin_recv, peer_send, peer_recv):
    rows, depth = hidden_ref.shape
    half = rows // HALVES
    vocab = head_ref.shape[1]
    tiles = pl.cdiv(vocab, 128)
    part_rows = 6 * half
    me = lax.axis_index("vp")
    group = lax.axis_index("dp")
    core = lax.rem(me, 2)
    chip = me // 2
    coords = (lax.rem(chip, SIDE), lax.rem(chip // SIDE, SIDE), chip // (SIDE * SIDE))
    sign = 1 - 2 * core
    partner = me + sign

    def device(there):
        return (group, there)

    def chip_at(offset):
        c = [lax.rem(coords[i] + sign * offset[i] + 2 * SIDE, SIDE) for i in range(3)]
        return (c[2] * SIDE + c[1]) * SIDE + c[0]

    def same_core(offset):
        return chip_at(offset) * 2 + core

    neighbours = [same_core(d) for d in DIRS]

    def behind(piece):
        return chip_at([-o for o in TREE[piece][2]])

    barrier = pltpu.get_barrier_semaphore()
    for there in (*neighbours, partner):
        pl.semaphore_signal(barrier, inc=1, device_id=device(there), device_id_type=MESH)
    own_head = pltpu.make_async_copy(head_ref, w_ref.at[0], w_sem)
    own_head.start()

    h = hidden_ref[...].astype(jnp.float32)
    inv_rms = lax.rsqrt(jnp.mean(h * h, axis=-1, keepdims=True) + NORM_EPS)
    normed = (h * inv_rms * gain_ref[...].astype(jnp.float32)).astype(jnp.bfloat16)
    for c in range(HALVES):
        x_ref[c, OWN] = normed[c * half : (c + 1) * half]

    pl.semaphore_wait(barrier, 7)

    def piece_copy(event, piece):
        d, parent, _ = TREE[piece]
        c = event % HALVES
        return pltpu.make_async_remote_copy(
            src_ref=x_ref.at[c, parent],
            dst_ref=x_ref.at[c, piece],
            send_sem=send_sem.at[event],
            recv_sem=recv_sem.at[event],
            device_id=device(neighbours[d]),
            device_id_type=MESH,
        )

    def send_event(event):
        for piece in pieces_of(event):
            piece_copy(event, piece).start()

    def event_bytes(event, sem):
        ps = pieces_of(event)
        block = x_ref.at[event % HALVES, ps.start : ps.stop]
        return pltpu.make_async_copy(block, block, sem.at[event])

    def stat_copy(piece):
        return pltpu.make_async_remote_copy(
            src_ref=mine_ref.at[piece // 2],
            dst_ref=stat_ref.at[piece],
            send_sem=stat_send,
            recv_sem=stat_recv,
            device_id=device(behind(piece) * 2 + core),
            device_id_type=MESH,
        )

    def send_stats(slot):
        for piece in pieces_of(HALVES * slot):
            stat_copy(piece).start()

    for event in range(HALVES):
        send_event(event)
    head_copy = pltpu.make_async_remote_copy(
        src_ref=head_ref, dst_ref=w_ref.at[1], send_sem=w_send, recv_sem=w_recv, device_id=device(partner), device_id_type=MESH
    )
    head_copy.start()

    def comm(event):
        slot = event // HALVES
        ahead = event + AHEAD
        if 2 * HALVES <= ahead < EVENTS:
            send_event(ahead)
        event_bytes(event, recv_sem).wait()
        if slot == 0:
            send_event(event + HALVES)
            if event + AHEAD < 2 * HALVES and False:
                pass
        if event % HALVES == 1 and slot >= 2:
            send_stats(slot - 2)

    lanes = lax.broadcasted_iota(jnp.int32, (half, 128), 1).astype(jnp.float32)
    eye_row = lax.broadcasted_iota(jnp.int32, (half, 128), 0)
    eye_lane = lax.broadcasted_iota(jnp.int32, (half, 128), 1)

    def targets(piece, source):
        row = target_ref[pl.ds(source, 1), :].astype(jnp.float32)
        for c in range(HALVES):
            hit = eye_lane == eye_row + (core * rows + c * half)
            column = jnp.sum(jnp.where(hit, row, 0.0), axis=1, keepdims=True)
            tgt_ref[c, piece] = column - lanes

    for piece in range(OWN):
        targets(piece, behind(piece))
    targets(OWN, chip)

    comm(0)
    comm(1)
    own_head.wait()
    head_copy.wait_recv()

    base = [(me * vocab).astype(jnp.float32), (partner * vocab).astype(jnp.float32)]
    lane_ids = lax.broadcasted_iota(jnp.int32, (half, 128), 1)
    last_ok = lane_ids < vocab - (tiles - 1) * 128

    def logits(x, at):
        n = x.shape[0]
        for b in range(2):
            z_ref[pl.ds(at, n), b * tiles * 128 : b * tiles * 128 + vocab] = jnp.dot(
                x, w_ref[b], preferred_element_type=jnp.float32
            )

    def strip_stats(at, c, piece, pack_at):
        def tile(b, k):
            return z_ref[pl.ds(at, half), (b * tiles + k) * 128 : (b * tiles + k + 1) * 128]

        def masked(k, v, other):
            return jnp.where(last_ok, v, other) if k == tiles - 1 else v

        top = tile(0, 0)
        for b in range(2):
            for k in range(tiles):
                top = jnp.maximum(top, masked(k, tile(b, k), LOW))
        total = jnp.zeros_like(top)
        moment = jnp.zeros_like(top)
        picked = jnp.zeros_like(top)
        for b in range(2):
            where = tgt_ref[c, piece] - base[b]
            for k in range(tiles):
                z = tile(b, k)
                shifted = z - top
                e = jnp.exp(shifted)
                total += masked(k, e, 0.0)
                moment += masked(k, e * shifted, 0.0)
                hit = where == float(128 * k)
                if k == tiles - 1:
                    hit = hit & last_ok
                picked = jnp.where(hit, z, picked)
        row_top = jnp.max(top, axis=1, keepdims=True)
        drop = top - row_top
        scale = jnp.exp(drop)
        row_moment = jnp.sum((moment + total * drop) * scale, axis=1, keepdims=True)
        row_total = jnp.sum(total * scale, axis=1, keepdims=True)
        row_picked = jnp.sum(picked, axis=1, keepdims=True)
        packed = jnp.where(lane_ids == 0, row_top, jnp.where(lane_ids == 1, row_total, jnp.where(lane_ids == 2, row_moment, row_picked)))
        pack_ref[pack_at, pl.ds(c * half, half), :] = packed

    def flush(pairs, first_pair):
        for i in range(pairs):
            block = pack_ref[2 * i : 2 * i + 2].reshape(2 * rows, 128)
            mine_ref[first_pair + i] = block.T[0:4, :]

    def compute(part):
        slot, c = part // HALVES, lax.rem(part, HALVES)
        x = x_ref[c, pl.ds(6 * slot, 6)].reshape(part_rows, depth)
        logits(x, 0)

        def strip(d, carry):
            strip_stats(pl.multiple_of(d * half, half), c, 6 * slot + d, d)
            return carry

        lax.fori_loop(0, 6, strip, 0)

        @pl.when(c == 1)
        def _():
            flush(3, 3 * slot)

    def step(part, carry):
        compute(part)
        for event in range(2, EVENTS):
            pl.when(part + 2 == event)(functools.partial(comm, event))
        return carry

    lax.fori_loop(0, 2 * FULL, step, 0)
    send_stats(FULL - 1)

    last = jnp.concatenate([x_ref[c, OWN - 3 : OWN + 1].reshape(4 * half, depth) for c in range(HALVES)], axis=0)
    logits(last, 0)
    for c in range(HALVES):

        def strip(d, carry, c=c):
            strip_stats(pl.multiple_of((4 * c + d) * half, half), c, OWN - 3 + d, d)
            return carry

        lax.fori_loop(0, 4, strip, 0)
    flush(2, 3 * FULL)
    send_stats(FULL)
    stat_ref[OWN] = mine_ref[OWN // 2]

    arrived = stat_ref.at[0:OWN]
    pltpu.make_async_copy(arrived, arrived, stat_recv).wait()
    piece_id = lax.broadcasted_iota(jnp.int32, (CHIPS, 128), 0)
    lane = lax.broadcasted_iota(jnp.int32, (CHIPS, 128), 1)
    ok = lax.rem(piece_id, 2) == lane // rows

    def folded(v, op):
        return op(v, pltpu.roll(v, rows, 1))

    tops = jnp.where(ok, stat_ref[:, 0, :], LOW)
    top = jnp.max(tops, axis=0, keepdims=True)
    top = folded(top, jnp.maximum)
    drop = tops - top
    scale = jnp.exp(drop)
    totals = stat_ref[:, 1, :]
    total = folded(jnp.sum(jnp.where(ok, totals * scale, 0.0), axis=0, keepdims=True), jnp.add)
    moments = (stat_ref[:, 2, :] + totals * drop) * scale
    moment = folded(jnp.sum(jnp.where(ok, moments, 0.0), axis=0, keepdims=True), jnp.add)
    picked = folded(jnp.sum(jnp.where(ok, stat_ref[:, 3, :], 0.0), axis=0, keepdims=True), jnp.add)
    log_total = jnp.log(total)
    mine = lax.broadcasted_iota(jnp.int32, (1, 128), 1) // rows == core
    res_ref[0:1, :] = jnp.where(mine, picked - top - log_total, 0.0)
    res_ref[1:2, :] = jnp.where(mine, log_total - moment / total, 0.0)
    fin_ref[chip] = res_ref[...]

    def fin_copy(there):
        return pltpu.make_async_remote_copy(
            src_ref=res_ref,
            dst_ref=fin_ref.at[chip],
            send_sem=fin_send,
            recv_sem=fin_recv,
            device_id=device(there * 2 + core),
            device_id_type=MESH,
        )

    def tell(i, carry):
        fin_copy(lax.rem(chip + i, CHIPS)).start()
        return carry

    lax.fori_loop(1, CHIPS, tell, 0)
    others = fin_ref.at[0 : CHIPS - 1]
    pltpu.make_async_copy(others, others, fin_recv).wait()
    across = pltpu.make_async_remote_copy(
        src_ref=fin_ref, dst_ref=peer_ref, send_sem=peer_send, recv_sem=peer_recv, device_id=device(partner), device_id_type=MESH
    )
    across.start()
    across.wait_recv()
    log_prob = fin_ref[:, 0, :] + peer_ref[:, 0, :]
    lp_ref[...] = log_prob
    ent_ref[...] = fin_ref[:, 1, :] + peer_ref[:, 1, :]
    mean_ref[0] = jnp.sum(log_prob) * (1.0 / (CHIPS * 2 * rows))

    across.wait_send()
    pltpu.make_async_copy(others, others, fin_send).wait()
    pltpu.make_async_copy(arrived, arrived, stat_send).wait()
    head_copy.wait_send()
    for event in range(EVENTS):
        event_bytes(event, send_sem).wait()


def solution(mesh):
    def local_step(hidden, target, norm_gain, head_weight):
        rows, depth = hidden.shape
        vocab = head_weight.shape[1]
        tiles = pl.cdiv(vocab, 128)
        half = rows // HALVES
        vmem = pl.BlockSpec(memory_space=pltpu.VMEM)
        dma = pltpu.SemaphoreType.DMA
        lp, ent, mean = pl.pallas_call(
            kernel,
            name="head",
            out_shape=(
                jax.ShapeDtypeStruct((CHIPS, 2 * rows), jnp.float32),
                jax.ShapeDtypeStruct((CHIPS, 2 * rows), jnp.float32),
                jax.ShapeDtypeStruct((1,), jnp.float32),
            ),
            in_specs=[vmem, vmem, vmem, pl.BlockSpec(memory_space=pl.ANY)],
            out_specs=(vmem, vmem, pl.BlockSpec(memory_space=pltpu.SMEM)),
            scratch_shapes=[
                pltpu.VMEM((HALVES, CHIPS, half, depth), jnp.bfloat16),
                pltpu.VMEM((2, depth, vocab), jnp.bfloat16),
                pltpu.VMEM((8 * half, 2 * tiles * 128), jnp.float32),
                pltpu.VMEM((HALVES, CHIPS, half, 128), jnp.float32),
                pltpu.VMEM((6, rows, 128), jnp.float32),
                pltpu.VMEM((CHIPS // 2, 4, 128), jnp.float32),
                pltpu.VMEM((CHIPS, 4, 128), jnp.float32),
                pltpu.VMEM((2, 128), jnp.float32),
                pltpu.VMEM((CHIPS, 2, 128), jnp.float32),
                pltpu.VMEM((CHIPS, 2, 128), jnp.float32),
                dma((EVENTS,)), dma((EVENTS,)), dma, dma, dma, dma, dma, dma, dma, dma, dma,
            ],
            compiler_params=pltpu.CompilerParams(
                collective_id=0, has_side_effects=True, vmem_limit_bytes=66_000_000
            ),
        )(hidden, norm_gain.reshape(1, depth), target.reshape(CHIPS, 2 * rows), head_weight)
        return lp.reshape(-1), ent.reshape(-1), mean

    return jax.shard_map(local_step, mesh=mesh, in_specs=(P(("dp", "vp"), None), P("dp"), P(None), P(None, "vp")), out_specs=(P("dp"), P("dp"), P("dp")), check_vma=False)
```

time: 485 us -> 167 us (0.34)
  waiting for transfers between devices: 296 us -> 0 us
  Pallas kernels: 0 us -> 148 us
  matrix products: 80.8 us -> 0 us
  blocking collectives: 64.5 us -> 0 us
  other arithmetic: 27.6 us -> 0 us
  local copies, waits for them, and re-layouts: 0 us -> 16.6 us
  between operations: 15.8 us -> 2.4 us
    all_gather x1 -> x0, waiting for transfers between devices: 152 us -> none  [local_step(): group_rows = lax.all_gather(normed, 'vp', axis=0, tiled=True)]
    pallas_call x0 -> x1, Pallas kernels: none -> 148 us  [local_step(): pl.pallas_call(kernel, name='head', out_shape=(jax.ShapeDtypeStruct((CHIP...]
    psum x1 -> x0, waiting for transfers between devices: 144 us -> none  [local_step(): row_stats = lax.psum(local_stats, 'vp')]
    dot_general x1 -> x0, matrix products: 80.8 us -> none  [local_step(): jnp.dot(group_rows, head_weight, preferred_element_type=jnp.float32)]
    pmax x1 -> x0, blocking collectives: 64.5 us -> none  [local_step(): row_max = lax.pmax(jnp.max(logits, axis=-1), 'vp')]
    reduce_sum x3 -> x0, other arithmetic: 23.4 us -> none  [the longest x1 19.8 us: local_step(): jnp.sum(exp_vals, axis=-1)]
    unnamed x0 -> x3, local copies, waits for them, and re-layouts: none -> 15.3 us
  transfers between devices with their start and end apart: 2 -> 0, of which waited for: 2 -> 0; matrix products, arithmetic and copies ran while one was open for 0% -> 0% of each run, Pallas kernels for 0% -> 0%
where the time goes in v1:
time: 167 us
  Pallas kernels  148 us (89%)
  local copies, waits for them, and re-layouts  16.6 us (10%)
  between operations  2.4 us (1%)
    pallas_call x1, Pallas kernels, local_step(): pl.pallas_call(kernel, name='head', out_shape=(jax.ShapeDtypeStruct((CHIP...  148 us
    unnamed x3, local copies, waits for them, and re-layouts  15.3 us

profile of v1, /device:TPU:1, one launch (start us, length us, event | category | flops | bytes accessed | tf_op | source)
XLA Modules:
  0.0 166.8 jit_solution(10969664503109654298)
XLA Ops:
  0.6 1.3 reshape.18.gain_ref
  1.9 12.6 %copy.7.head_ref = bf16[3584,1187]{1,0:T(8,128)(2,1)} copy(bf16[3584,1187]{0,1:T(8,128)(2,1)} %param.7) | data formatting | bytes 17016832 | tf_op args[3]
  14.5 147.8 %head.1 = (f32[64,128]{1,0:T(8,128)}, f32[64,128]{1,0:T(8,128)}, f32[1]{0:T(128)}) custom-call(bf16[64,3584]{1,0:T(8,128)(2,1)} %hidden_ref.1, bf16[1,3584]{1,0:T(2,128)(2,1)} %reshape.18.gain_ref, s32[64,128]{1,0:T(8,128)} %bitcast.3, bf16[3584,1187]{1,0:T(8,128)(2,1)} %copy.7.head_ref), custom_call_target="tpu_custom_call" | custom-call | tf_op jit(solution)/shard_map/head/pallas_call | solution.py:318
  162.3 1.4 copy.11
  163.7 1.4 copy.12

commit v2 on v1

v2 whole, which is shorter than its diff:
```python
import functools

import jax
import jax.numpy as jnp
from jax import lax
from jax.experimental import pallas as pl
from jax.experimental.pallas import tpu as pltpu
from jax.sharding import PartitionSpec as P

NORM_EPS = 1e-6
MESH = pl.DeviceIdType.MESH
SIDE = 4
CHIPS = SIDE**3
OWN = CHIPS - 1
LOW = -3.0e38
DIRS = ((1, 0, 0), (0, 1, 0), (0, 0, 1), (-1, 0, 0), (0, -1, 0), (0, 0, -1))
FULL = 10

PARENT = (
    63, 63, 63, 63, 63, 63, 4, 0, 4, 3, 4, 0, 2, 3, 3, 4, 5, 5, 7, 2, 6, 5, 9, 1, 11, 17, 12, 16, 11, 16, 10, 19,
    9, 8, 16, 7, 26, 12, 14, 19, 15, 13, 35, 18, 30, 29, 28, 35, 28, 36, 31, 31, 26, 41, 46, 41, 43, 39, 32, 46, 52, 49, 51,
)
HALVES = 2
EVENTS = HALVES * (FULL + 1)
GROUPS = EVENTS
AHEAD = 4
STAGES = 4
WIDE = 512


def offsets():
    out = {OWN: (0, 0, 0)}
    for j, parent in enumerate(PARENT):
        out[j] = tuple((a + b) % SIDE for a, b in zip(out[parent], DIRS[j % 6]))
    return out


OFFSET = offsets()


def pieces_of(slot):
    return range(6 * slot, min(6 * slot + 6, OWN))


def place(piece, c):
    if piece == OWN:
        return GROUPS - 1, c
    if piece >= 6 * FULL:
        return HALVES * FULL, piece - 6 * FULL + 3 * c
    return HALVES * (piece // 6) + c, piece % 6


def kernel(hidden_ref, gain_ref, target_ref, head_ref, lp_ref, ent_ref, mean_ref, x_ref, w_ref, stage_ref, rest_ref, za_ref, zb_ref,
           tgt_ref, pack_ref, mine_ref, stat_ref, res_ref, fin_ref, peer_ref, send_sem, recv_sem, stage_sem, rest_sem, w_send, w_recv,
           stat_send, stat_recv, fin_send, fin_recv, peer_send, peer_recv):
    rows, depth = hidden_ref.shape
    half = rows // HALVES
    vocab = head_ref.shape[0]
    tiles = pl.cdiv(vocab, 128)
    width = tiles * 128
    me = lax.axis_index("vp")
    group = lax.axis_index("dp")
    core = lax.rem(me, 2)
    chip = me // 2
    coords = (lax.rem(chip, SIDE), lax.rem(chip // SIDE, SIDE), chip // (SIDE * SIDE))
    sign = 1 - 2 * core
    partner = me + sign

    def device(there):
        return (group, there)

    def chip_at(offset):
        c = [lax.rem(coords[i] + sign * offset[i] + 2 * SIDE, SIDE) for i in range(3)]
        return (c[2] * SIDE + c[1]) * SIDE + c[0]

    neighbours = [chip_at(d) * 2 + core for d in DIRS]

    def behind(piece):
        return chip_at([-o for o in OFFSET[piece]])

    barrier = pltpu.get_barrier_semaphore()
    for there in (*neighbours, partner):
        pl.semaphore_signal(barrier, inc=1, device_id=device(there), device_id_type=MESH)

    def stage_copy(n):
        return pltpu.make_async_copy(head_ref.at[128 * n : 128 * n + 128], stage_ref.at[n % STAGES], stage_sem.at[n % STAGES])

    whole = vocab // 128
    for n in range(STAGES):
        stage_copy(n).start()
    rest_copy = pltpu.make_async_copy(head_ref.at[128 * whole : vocab], rest_ref, rest_sem)
    rest_copy.start()

    h = hidden_ref[...].astype(jnp.float32)
    inv_rms = lax.rsqrt(jnp.mean(h * h, axis=-1, keepdims=True) + NORM_EPS)
    normed = (h * inv_rms * gain_ref[...].astype(jnp.float32)).astype(jnp.bfloat16)
    for c in range(HALVES):
        x_ref[GROUPS - 1, c] = normed[c * half : (c + 1) * half]

    pl.semaphore_wait(barrier, 7)

    def send_event(event):
        c = event % HALVES
        for piece in pieces_of(event // HALVES):
            pltpu.make_async_remote_copy(
                src_ref=x_ref.at[place(PARENT[piece], c)],
                dst_ref=x_ref.at[place(piece, c)],
                send_sem=send_sem.at[event],
                recv_sem=recv_sem.at[event],
                device_id=device(neighbours[piece % 6]),
                device_id_type=MESH,
            ).start()

    def wait_event(event, sem):
        ps = pieces_of(event // HALVES)
        g, d = place(ps.start, event % HALVES)
        block = x_ref.at[g, d : d + len(ps)]
        pltpu.make_async_copy(block, block, sem.at[event]).wait()

    for event in range(HALVES):
        send_event(event)

    def head_copy(n):
        return pltpu.make_async_remote_copy(
            src_ref=w_ref.at[:, 128 * n : 128 * n + 128],
            dst_ref=w_ref.at[:, width + 128 * n : width + 128 * n + 128],
            send_sem=w_send,
            recv_sem=w_recv,
            device_id=device(partner),
            device_id_type=MESH,
        )

    for n in range(tiles):
        if n < whole:
            stage_copy(n).wait()
        else:
            rest_copy.wait()
            stage_ref[n % STAGES, 0 : vocab - 128 * whole] = rest_ref[...]

        def turn(k, carry, n=n):
            for u in range(4):
                at = pl.multiple_of((4 * k + u) * 128, 128)
                w_ref[pl.ds(at, 128), 128 * n : 128 * n + 128] = stage_ref[n % STAGES, :, pl.ds(at, 128)].T
            return carry

        lax.fori_loop(0, depth // 512, turn, 0)
        if n + STAGES < whole:
            stage_copy(n + STAGES).start()
        if n:
            head_copy(n - 1).start()

    lane_ids = lax.broadcasted_iota(jnp.int32, (half, 128), 1)
    row_ids = lax.broadcasted_iota(jnp.int32, (half, 128), 0)
    lanes = lane_ids.astype(jnp.float32)
    last_ok = lane_ids < vocab - (tiles - 1) * 128

    def targets(piece):
        row = target_ref[pl.ds(behind(piece), 1), :].astype(jnp.float32)
        for c in range(HALVES):
            hit = lane_ids == row_ids + (core * rows + c * half)
            column = jnp.sum(jnp.where(hit, row, 0.0), axis=1, keepdims=True)
            tgt_ref[place(piece, c)] = column - lanes

    for piece in range(CHIPS):
        targets(piece)
        if piece == 0:
            head_copy(tiles - 1).start()

    def comm(event):
        wait_event(event, recv_sem)
        if event < HALVES:
            send_event(event + HALVES)
        if event + AHEAD < EVENTS:
            send_event(event + AHEAD)

    comm(0)
    comm(1)
    partner_head = w_ref.at[:, width : 2 * width]
    pltpu.make_async_copy(partner_head, partner_head, w_recv).wait()

    base = [(me * vocab).astype(jnp.float32), (partner * vocab).astype(jnp.float32)]

    def strip_stats(z_ref, g, d, pack_at):
        def tile(b, k):
            return z_ref[d * half : (d + 1) * half, (b * tiles + k) * 128 : (b * tiles + k + 1) * 128]

        def masked(k, v, other):
            return jnp.where(last_ok, v, other) if k == tiles - 1 else v

        top = tile(0, 0)
        for b in range(2):
            for k in range(tiles):
                top = jnp.maximum(top, masked(k, tile(b, k), LOW))
        total = jnp.zeros_like(top)
        moment = jnp.zeros_like(top)
        picked = jnp.zeros_like(top)
        for b in range(2):
            where = tgt_ref[g, d] - base[b]
            for k in range(tiles):
                z = tile(b, k)
                shifted = z - top
                e = jnp.exp(shifted)
                total += masked(k, e, 0.0)
                moment += masked(k, e * shifted, 0.0)
                hit = where == float(128 * k)
                if k == tiles - 1:
                    hit = hit & last_ok
                picked = jnp.where(hit, z, picked)
        row_top = jnp.max(top, axis=1, keepdims=True)
        drop = top - row_top
        scale = jnp.exp(drop)
        row_moment = jnp.sum((moment + total * drop) * scale, axis=1, keepdims=True)
        row_total = jnp.sum(total * scale, axis=1, keepdims=True)
        row_picked = jnp.sum(picked, axis=1, keepdims=True)
        packed = jnp.where(lane_ids == 0, row_top, jnp.where(lane_ids == 1, row_total, jnp.where(lane_ids == 2, row_moment, row_picked)))
        pack_ref[pack_at] = packed

    def part(g, z_ref, before, other_ref, pack_at):
        x = x_ref[g].reshape(6 * half, depth)
        for n in range(2 * width // WIDE):
            at = slice(n * WIDE, (n + 1) * WIDE)
            z_ref[:, at] = jnp.dot(x, w_ref[:, at], preferred_element_type=jnp.float32)
            strip_stats(other_ref, before, n, pack_at(n))
        for d in range(2 * width // WIDE, 6):
            strip_stats(other_ref, before, d, pack_at(d))

    def flush(pairs, first_pair):
        for i in range(pairs):
            block = pack_ref[4 * i : 4 * i + 4].reshape(2 * rows, 128)
            mine_ref[first_pair + i] = block.T[0:4, :]

    def stat_copy(piece):
        return pltpu.make_async_remote_copy(
            src_ref=mine_ref.at[piece // 2],
            dst_ref=stat_ref.at[piece],
            send_sem=stat_send,
            recv_sem=stat_recv,
            device_id=device(behind(piece) * 2 + core),
            device_id_type=MESH,
        )

    def send_stats(slot):
        for piece in pieces_of(slot):
            stat_copy(piece).start()

    def at_turn(turn, first, last, what):
        for t in range(first, last):
            pl.when(turn == t)(functools.partial(what, t))

    def step(turn, carry):
        def before_first(t):
            comm(2 * t - 1)

        def before_second(t):
            comm(2 * t)
            if t == FULL:
                comm(2 * t + 1)
            if t >= 2:
                send_stats(t - 2)

        at_turn(turn, 2, FULL + 1, before_first)
        first = jnp.where(turn == 0, GROUPS - 1, 2 * turn - 1)
        part(first, za_ref, jnp.maximum(2 * turn - 2, 0), zb_ref, lambda d: 2 * d)
        at_turn(turn, 1, FULL + 1, before_second)
        part(2 * turn, zb_ref, first, za_ref, lambda d: jnp.where(turn == 0, d, 2 * d + 1))

        @pl.when(turn > 0)
        def _():
            flush(3, 3 * (turn - 1))

        @pl.when(turn == 0)
        def _():
            pack_ref[2] = pack_ref[0]
            pack_ref[3] = pack_ref[1]
            flush(1, OWN // 2)
            stat_ref[OWN] = mine_ref[OWN // 2]

        return carry

    lax.fori_loop(0, FULL + 1, step, 0)
    send_stats(FULL - 1)
    for d in range(6):
        strip_stats(zb_ref, HALVES * FULL, d, 2 * (d % 3) + d // 3)
    flush(2, 3 * FULL)
    send_stats(FULL)

    arrived = stat_ref.at[0:OWN]
    pltpu.make_async_copy(arrived, arrived, stat_recv).wait()
    piece_id = lax.broadcasted_iota(jnp.int32, (CHIPS, 128), 0)
    lane = lax.broadcasted_iota(jnp.int32, (CHIPS, 128), 1)
    ok = lax.rem(piece_id, 2) == lane // rows

    def folded(v, op):
        return op(v, pltpu.roll(v, rows, 1))

    tops = jnp.where(ok, stat_ref[:, 0, :], LOW)
    top = jnp.max(tops, axis=0, keepdims=True)
    top = folded(top, jnp.maximum)
    drop = tops - top
    scale = jnp.exp(drop)
    totals = stat_ref[:, 1, :]
    total = folded(jnp.sum(jnp.where(ok, totals * scale, 0.0), axis=0, keepdims=True), jnp.add)
    moments = (stat_ref[:, 2, :] + totals * drop) * scale
    moment = folded(jnp.sum(jnp.where(ok, moments, 0.0), axis=0, keepdims=True), jnp.add)
    picked = folded(jnp.sum(jnp.where(ok, stat_ref[:, 3, :], 0.0), axis=0, keepdims=True), jnp.add)
    log_total = jnp.log(total)
    mine = lax.broadcasted_iota(jnp.int32, (1, 128), 1) // rows == core
    res_ref[0:1, :] = jnp.where(mine, picked - top - log_total, 0.0)
    res_ref[1:2, :] = jnp.where(mine, log_total - moment / total, 0.0)
    fin_ref[chip] = res_ref[...]

    def fin_copy(there):
        return pltpu.make_async_remote_copy(
            src_ref=res_ref,
            dst_ref=fin_ref.at[chip],
            send_sem=fin_send,
            recv_sem=fin_recv,
            device_id=device(there * 2 + core),
            device_id_type=MESH,
        )

    def tell(i, carry):
        fin_copy(lax.rem(chip + i, CHIPS)).start()
        return carry

    lax.fori_loop(1, CHIPS, tell, 0)
    others = fin_ref.at[0 : CHIPS - 1]
    pltpu.make_async_copy(others, others, fin_recv).wait()
    across = pltpu.make_async_remote_copy(
        src_ref=fin_ref, dst_ref=peer_ref, send_sem=peer_send, recv_sem=peer_recv, device_id=device(partner), device_id_type=MESH
    )
    across.start()
    across.wait_recv()
    log_prob = fin_ref[:, 0, :] + peer_ref[:, 0, :]
    lp_ref[...] = log_prob
    ent_ref[...] = fin_ref[:, 1, :] + peer_ref[:, 1, :]
    mean_ref[0] = jnp.sum(log_prob) * (1.0 / (CHIPS * 2 * rows))

    across.wait_send()
    pltpu.make_async_copy(others, others, fin_send).wait()
    pltpu.make_async_copy(arrived, arrived, stat_send).wait()
    pltpu.make_async_copy(partner_head, partner_head, w_send).wait()
    for event in range(EVENTS):
        wait_event(event, send_sem)


def solution(mesh):
    def local_step(hidden, target, norm_gain, head_weight):
        rows, depth = hidden.shape
        vocab = head_weight.shape[1]
        width = pl.cdiv(vocab, 128) * 128
        half = rows // HALVES
        vmem = pl.BlockSpec(memory_space=pltpu.VMEM)
        dma = pltpu.SemaphoreType.DMA
        lp, ent, mean = pl.pallas_call(
            kernel,
            name="head",
            out_shape=(
                jax.ShapeDtypeStruct((CHIPS, 2 * rows), jnp.float32),
                jax.ShapeDtypeStruct((CHIPS, 2 * rows), jnp.float32),
                jax.ShapeDtypeStruct((1,), jnp.float32),
            ),
            in_specs=[vmem, vmem, vmem, pl.BlockSpec(memory_space=pl.ANY)],
            out_specs=(vmem, vmem, pl.BlockSpec(memory_space=pltpu.SMEM)),
            scratch_shapes=[
                pltpu.VMEM((GROUPS, 6, half, depth), jnp.bfloat16),
                pltpu.VMEM((depth, 2 * width), jnp.bfloat16),
                pltpu.VMEM((STAGES, 128, depth), jnp.bfloat16),
                pltpu.VMEM((vocab % 128, depth), jnp.bfloat16),
                pltpu.VMEM((6 * half, 2 * width), jnp.float32),
                pltpu.VMEM((6 * half, 2 * width), jnp.float32),
                pltpu.VMEM((GROUPS, 6, half, 128), jnp.float32),
                pltpu.VMEM((12, half, 128), jnp.float32),
                pltpu.VMEM((CHIPS // 2, 4, 128), jnp.float32),
                pltpu.VMEM((CHIPS, 4, 128), jnp.float32),
                pltpu.VMEM((2, 128), jnp.float32),
                pltpu.VMEM((CHIPS, 2, 128), jnp.float32),
                pltpu.VMEM((CHIPS, 2, 128), jnp.float32),
                dma((EVENTS,)), dma((EVENTS,)), dma((STAGES,)), dma, dma, dma, dma, dma, dma, dma, dma, dma,
            ],
            compiler_params=pltpu.CompilerParams(
                collective_id=0, has_side_effects=True, vmem_limit_bytes=67_000_000
            ),
        )(hidden, norm_gain, target.reshape(CHIPS, 2 * rows), head_weight.T)
        return lp.reshape(-1), ent.reshape(-1), mean

    return jax.shard_map(local_step, mesh=mesh, in_specs=(P(("dp", "vp"), None), P("dp"), P(None), P(None, "vp")), out_specs=(P("dp"), P("dp"), P("dp")), check_vma=False)
```

time: 167 us -> 139 us (0.83)
  Pallas kernels: 148 us -> 134 us
  local copies, waits for them, and re-layouts: 16.6 us -> 2.75 us
    pallas_call x1, Pallas kernels: 148 us -> 134 us  [local_step(): pl.pallas_call(kernel, name='head', out_shape=(jax.ShapeDtypeStruct((CHIP...]
    unnamed x3 -> x2, local copies, waits for them, and re-layouts: 15.3 us -> 2.75 us
where the time goes in v2:
time: 139 us
  Pallas kernels  134 us (96%)
  local copies, waits for them, and re-layouts  2.75 us (2%)
  between operations  2.39 us (2%)
    pallas_call x1, Pallas kernels, local_step(): pl.pallas_call(kernel, name='head', out_shape=(jax.ShapeDtypeStruct((CHIP...  134 us

profile of v2, /device:TPU:1, one launch (start us, length us, event | category | flops | bytes accessed | tf_op | source)
XLA Modules:
  0.0 138.9 jit_solution(6499311106582891875)
XLA Ops:
  0.6 133.8 %head.1 = (f32[64,128]{1,0:T(8,128)}, f32[64,128]{1,0:T(8,128)}, f32[1]{0:T(128)}) custom-call(bf16[64,3584]{1,0:T(8,128)(2,1)} %hidden_ref.1, bf16[3584]{0:T(1024)(128)(2,1)} %gain_ref.1, s32[64,128]{1,0:T(8,128)} %bitcast.5, bf16[1187,3584]{1,0:T(8,128)(2,1)} %bitcast.4), custom_call_target="tpu_custom_call" | custom-call | tf_op jit(solution)/shard_map/head/pallas_call | solution.py:355
  134.4 1.4 copy.10
  135.8 1.4 copy.11

commit v3 on v2

--- a/solution.py
+++ b/solution.py
@@ -1,4 +1,5 @@
 import functools
+import itertools
 
 import jax
 import jax.numpy as jnp
@@ -36,6 +37,7 @@
 
 
 OFFSET = offsets()
+FARTHEST = (SIDE // 2,) * 3
 
 
 def pieces_of(slot):
@@ -50,9 +52,9 @@
     return HALVES * (piece // 6) + c, piece % 6
 
 
-def kernel(hidden_ref, gain_ref, target_ref, head_ref, lp_ref, ent_ref, mean_ref, x_ref, w_ref, stage_ref, rest_ref, za_ref, zb_ref,
-           tgt_ref, pack_ref, mine_ref, stat_ref, res_ref, fin_ref, peer_ref, send_sem, recv_sem, stage_sem, rest_sem, w_send, w_recv,
-           stat_send, stat_recv, fin_send, fin_recv, peer_send, peer_recv):
+def kernel(hidden_ref, gain_ref, target_ref, head_ref, out_ref, mean_ref, x_ref, w_ref, stage_ref, rest_ref, za_ref, zb_ref,
+           tgt_ref, pack_ref, mine_ref, stat_ref, res_ref, fin_ref, send_sem, recv_sem, stage_sem, rest_sem, w_send, w_recv,
+           stat_send, stat_recv, fin_send, fin_recv):
     rows, depth = hidden_ref.shape
     half = rows // HALVES
     vocab = head_ref.shape[0]
@@ -77,6 +79,9 @@
 
     def behind(piece):
         return chip_at([-o for o in OFFSET[piece]])
+
+    def merger(piece):
+        return chip_at([SIDE // 2 - o for o in OFFSET[piece]])
 
     barrier = pltpu.get_barrier_semaphore()
     for there in (*neighbours, partner):
@@ -231,17 +236,20 @@
 
     def stat_copy(piece):
         return pltpu.make_async_remote_copy(
-            src_ref=mine_ref.at[piece // 2],
+            src_ref=mine_ref.at[CHIPS // 2 if piece == OWN else piece // 2],
             dst_ref=stat_ref.at[piece],
             send_sem=stat_send,
             recv_sem=stat_recv,
-            device_id=device(behind(piece) * 2 + core),
+            device_id=device(merger(piece) * 2 + core),
             device_id_type=MESH,
         )
 
-    def send_stats(slot):
-        for piece in pieces_of(slot):
-            stat_copy(piece).start()
+    def send_stats(pieces):
+        for piece in pieces:
+            if OFFSET[piece] == FARTHEST:
+                stat_ref[piece] = mine_ref[piece // 2]
+            else:
+                stat_copy(piece).start()
 
     def at_turn(turn, first, last, what):
         for t in range(first, last):
@@ -255,8 +263,12 @@
             comm(2 * t)
             if t == FULL:
                 comm(2 * t + 1)
-            if t >= 2:
-                send_stats(t - 2)
+            if t == FULL - 2:
+                send_stats([*range(18), OWN])
+            if t == FULL - 1:
+                send_stats(range(18, 42))
+            if t == FULL:
+                send_stats(range(42, 54))
 
         at_turn(turn, 2, FULL + 1, before_first)
         first = jnp.where(turn == 0, GROUPS - 1, 2 * turn - 1)
@@ -272,19 +284,18 @@
         def _():
             pack_ref[2] = pack_ref[0]
             pack_ref[3] = pack_ref[1]
-            flush(1, OWN // 2)
-            stat_ref[OWN] = mine_ref[OWN // 2]
+            flush(1, CHIPS // 2)
 
         return carry
 
     lax.fori_loop(0, FULL + 1, step, 0)
-    send_stats(FULL - 1)
+    send_stats(pieces_of(FULL - 1))
     for d in range(6):
         strip_stats(zb_ref, HALVES * FULL, d, 2 * (d % 3) + d // 3)
     flush(2, 3 * FULL)
-    send_stats(FULL)
-
-    arrived = stat_ref.at[0:OWN]
+    send_stats(pieces_of(FULL))
+
+    arrived = stat_ref.at[0 : CHIPS - 1]
     pltpu.make_async_copy(arrived, arrived, stat_recv).wait()
     piece_id = lax.broadcasted_iota(jnp.int32, (CHIPS, 128), 0)
     lane = lax.broadcasted_iota(jnp.int32, (CHIPS, 128), 1)
@@ -307,36 +318,34 @@
     mine = lax.broadcasted_iota(jnp.int32, (1, 128), 1) // rows == core
     res_ref[0:1, :] = jnp.where(mine, picked - top - log_total, 0.0)
     res_ref[1:2, :] = jnp.where(mine, log_total - moment / total, 0.0)
-    fin_ref[chip] = res_ref[...]
-
-    def fin_copy(there):
-        return pltpu.make_async_remote_copy(
-            src_ref=res_ref,
-            dst_ref=fin_ref.at[chip],
-            send_sem=fin_send,
-            recv_sem=fin_recv,
-            device_id=device(there * 2 + core),
-            device_id_type=MESH,
-        )
-
-    def tell(i, carry):
-        fin_copy(lax.rem(chip + i, CHIPS)).start()
-        return carry
-
-    lax.fori_loop(1, CHIPS, tell, 0)
-    others = fin_ref.at[0 : CHIPS - 1]
+
+    origin = core * CHIPS + merger(OWN)
+    fin_ref[origin] = res_ref[...]
+    steps = [[lax.rem(coords[i] + k, SIDE) for k in range(SIDE)] for i in range(3)]
+
+    def hops(offset):
+        return sum(min(o, SIDE - o) for o in offset)
+
+    for x, y, z in sorted(itertools.product(range(SIDE), repeat=3), key=hops, reverse=True):
+        there = ((steps[2][z] * SIDE + steps[1][y]) * SIDE + steps[0][x]) * 2
+        for side in range(2):
+            if hops((x, y, z)) == 0 and side == 1:
+                continue
+            pltpu.make_async_remote_copy(
+                src_ref=res_ref,
+                dst_ref=fin_ref.at[origin],
+                send_sem=fin_send,
+                recv_sem=fin_recv,
+                device_id=device(partner if hops((x, y, z)) == 0 else there + side),
+                device_id_type=MESH,
+            ).start()
+    others = fin_ref.at[0 : 2 * CHIPS - 1]
     pltpu.make_async_copy(others, others, fin_recv).wait()
-    across = pltpu.make_async_remote_copy(
-        src_ref=fin_ref, dst_ref=peer_ref, send_sem=peer_send, recv_sem=peer_recv, device_id=device(partner), device_id_type=MESH
-    )
-    across.start()
-    across.wait_recv()
-    log_prob = fin_ref[:, 0, :] + peer_ref[:, 0, :]
-    lp_ref[...] = log_prob
-    ent_ref[...] = fin_ref[:, 1, :] + peer_ref[:, 1, :]
+    log_prob = fin_ref[0:CHIPS, 0, :] + fin_ref[CHIPS:, 0, :]
+    out_ref[0] = log_prob
+    out_ref[1] = fin_ref[0:CHIPS, 1, :] + fin_ref[CHIPS:, 1, :]
     mean_ref[0] = jnp.sum(log_prob) * (1.0 / (CHIPS * 2 * rows))
 
-    across.wait_send()
     pltpu.make_async_copy(others, others, fin_send).wait()
     pltpu.make_async_copy(arrived, arrived, stat_send).wait()
     pltpu.make_async_copy(partner_head, partner_head, w_send).wait()
@@ -352,16 +361,15 @@
         half = rows // HALVES
         vmem = pl.BlockSpec(memory_space=pltpu.VMEM)
         dma = pltpu.SemaphoreType.DMA
-        lp, ent, mean = pl.pallas_call(
+        out, mean = pl.pallas_call(
             kernel,
             name="head",
             out_shape=(
-                jax.ShapeDtypeStruct((CHIPS, 2 * rows), jnp.float32),
-                jax.ShapeDtypeStruct((CHIPS, 2 * rows), jnp.float32),
+                jax.ShapeDtypeStruct((2, CHIPS, 2 * rows), jnp.float32),
                 jax.ShapeDtypeStruct((1,), jnp.float32),
             ),
             in_specs=[vmem, vmem, vmem, pl.BlockSpec(memory_space=pl.ANY)],
-            out_specs=(vmem, vmem, pl.BlockSpec(memory_space=pltpu.SMEM)),
+            out_specs=(vmem, pl.BlockSpec(memory_space=pltpu.SMEM)),
             scratch_shapes=[
                 pltpu.VMEM((GROUPS, 6, half, depth), jnp.bfloat16),
                 pltpu.VMEM((depth, 2 * width), jnp.bfloat16),
@@ -371,17 +379,16 @@
                 pltpu.VMEM((6 * half, 2 * width), jnp.float32),
                 pltpu.VMEM((GROUPS, 6, half, 128), jnp.float32),
                 pltpu.VMEM((12, half, 128), jnp.float32),
-                pltpu.VMEM((CHIPS // 2, 4, 128), jnp.float32),
+                pltpu.VMEM((CHIPS // 2 + 1, 4, 128), jnp.float32),
                 pltpu.VMEM((CHIPS, 4, 128), jnp.float32),
                 pltpu.VMEM((2, 128), jnp.float32),
-                pltpu.VMEM((CHIPS, 2, 128), jnp.float32),
-                pltpu.VMEM((CHIPS, 2, 128), jnp.float32),
-                dma((EVENTS,)), dma((EVENTS,)), dma((STAGES,)), dma, dma, dma, dma, dma, dma, dma, dma, dma,
+                pltpu.VMEM((2 * CHIPS, 2, 128), jnp.float32),
+                dma((EVENTS,)), dma((EVENTS,)), dma((STAGES,)), dma, dma, dma, dma, dma, dma, dma,
             ],
             compiler_params=pltpu.CompilerParams(
                 collective_id=0, has_side_effects=True, vmem_limit_bytes=67_000_000
             ),
         )(hidden, norm_gain, target.reshape(CHIPS, 2 * rows), head_weight.T)
-        return lp.reshape(-1), ent.reshape(-1), mean
+        return out[0].reshape(-1), out[1].reshape(-1), mean
 
     return jax.shard_map(local_step, mesh=mesh, in_specs=(P(("dp", "vp"), None), P("dp"), P(None), P(None, "vp")), out_specs=(P("dp"), P("dp"), P("dp")), check_vma=False)

time: 139 us -> 135 us (0.971)
  Pallas kernels: 134 us -> 131 us
    pallas_call x1, Pallas kernels: 134 us -> 131 us  [local_step(): pl.pallas_call(kernel, name='head', out_shape=(jax.ShapeDtypeStruct((2, C...]
    unnamed x2 -> x0, local copies, waits for them, and re-layouts: 2.75 us -> none
    another operation x0 -> x1, local copies, waits for them, and re-layouts: none -> 1.4 us  [local_step(): return (out[0].reshape(-1), out[1].reshape(-1), mean)]
where the time goes in v3:
time: 135 us; the launch traced here: 134 us
  Pallas kernels  131 us (97%)
  between operations  2.33 us (2%)
  local copies, waits for them, and re-layouts  1.4 us (1%)
    pallas_call x1, Pallas kernels, local_step(): pl.pallas_call(kernel, name='head', out_shape=(jax.ShapeDtypeStruct((2, C...  131 us

profile of v3, /device:TPU:1, one launch (start us, length us, event | category | flops | bytes accessed | tf_op | source)
XLA Modules:
  0.0 134.4 jit_solution(17363437485658124553)
XLA Ops:
  0.6 130.6 %head.1 = (f32[2,64,128]{2,1,0:T(8,128)}, f32[1]{0:T(128)}) custom-call(bf16[64,3584]{1,0:T(8,128)(2,1)} %hidden_ref.1, bf16[3584]{0:T(1024)(128)(2,1)} %gain_ref.1, s32[64,128]{1,0:T(8,128)} %bitcast.7, bf16[1187,3584]{1,0:T(8,128)(2,1)} %bitcast.6), custom_call_target="tpu_custom_call" | custom-call | tf_op jit(solution)/shard_map/head/pallas_call | solution.py:364
  131.3 1.4 %slice_bitcast_fusion = (f32[8192]{0:T(1024)}, f32[8192]{0:T(1024)}) fusion(f32[2,64,128]{2,1,0:T(8,128)} %get-tuple-element.5), kind=kLoop, calls=%fused_computation | loop fusion | bytes 131072 | tf_op jit(solution)/shard_map/reshape;squeeze | solution.py:392
